TPU v7x, 32 devices: a whole 2x2x4 slice. The times are simulated.
32 devices in a mesh: dp: 4 (over z), rows: 8 (over y, x, core).
Axes of the slice: x: 2, y: 2, z: 4, core: 2. Of those that a mesh axis runs over, the one named last changes fastest.
Arguments:
- latent: bfloat16 [8, 8, 64, 640], P('dp', 'rows'), may hold values from -16.25 to 16.25
- hidden: bfloat16 [8, 8, 64, 640], P('dp', 'rows'), may hold values from -16.25 to 16.25
- cotangent: bfloat16 [8, 8, 64, 640], P('dp', 'rows'), may hold values from -6 to 6
- filter_one: bfloat16 [9, 640, 640], P(None, 'dp', 'rows'), may hold values from -0.078125 to 0.078125
- filter_two: bfloat16 [9, 640, 640], P(None, 'dp', 'rows'), may hold values from -0.078125 to 0.078125
- gain_one: float32 [640], replicated, may hold values from 0.1 to 1.9
- shift_one: float32 [640], replicated, may hold values from -2.5 to 2.5
- gain_two: float32 [640], replicated, may hold values from 0.1 to 1.9
- shift_two: float32 [640], replicated, may hold values from -2.5 to 2.5
Outputs:
- latent_grad: bfloat16 [8, 8, 64, 640], P('dp', 'rows')
All inputs are finite; a program needn't handle non-finite values.
Results may differ from a plain program's by a relative error of at most 0.0027.
Values may be sent and summed in bfloat16 or wider, within the bound.
A program may use at most 128 MiB of HBM per device.

v0:
```python
import jax
import jax.numpy as jnp
from jax import lax
from jax.sharding import PartitionSpec as P

GROUPS = 16
GSIZE = 40


def extended(block, sides, width):
    for axis, dim in sides:
        count = lax.axis_size(axis)
        forward = [(i, i + 1) for i in range(count - 1)]
        backward = [(target, source) for source, target in forward]
        low = lax.ppermute(
            lax.slice_in_dim(block, block.shape[dim] - width, None, axis=dim), axis, forward
        )
        high = lax.ppermute(lax.slice_in_dim(block, 0, width, axis=dim), axis, backward)
        block = jnp.concatenate([low, block, high], axis=dim)
    return block


def group_sums(values):
    per_channel = jnp.sum(values, axis=(1, 2))
    return jnp.sum(per_channel.reshape(per_channel.shape[0], GROUPS, -1), axis=2)


def expand_groups(moment):
    return jnp.repeat(moment, GSIZE, axis=1)[:, None, None, :]


def finish_stats(sum_plain, sum_square, number):
    average = sum_plain / number
    variance = sum_square / number - average * average
    return (average, lax.rsqrt(variance + 1e-05))


def reduced_stats(field, number):
    values = field.astype(jnp.float32)
    sum_plain, sum_square = lax.psum((group_sums(values), group_sums(values * values)), "rows")
    return finish_stats(sum_plain, sum_square, number)


def norm_backward(field, stats, gain, shift, incoming, number):
    average, inverse = stats
    values = field.astype(jnp.float32)
    normed = (values - expand_groups(average)) * expand_groups(inverse)
    linear = normed * gain + shift
    logistic = jax.nn.sigmoid(linear)
    scaled = incoming * logistic * (1.0 + linear * (1.0 - logistic)) * gain
    sum_first, sum_second = lax.psum((group_sums(scaled), group_sums(scaled * normed)), "rows")
    first = sum_first / number
    second = sum_second / number
    return expand_groups(inverse) * (scaled - expand_groups(first) - normed * expand_groups(second))


def conv_backward(gradient, weights):
    images, rows_here, breadth, channels = gradient.shape
    padded = extended(gradient, (("rows", 1),), 1)
    padded = jnp.pad(padded, ((0, 0), (0, 0), (1, 1), (0, 0)))
    pixels = images * rows_here * breadth
    shifted = []
    for tap_index in range(9):
        down_step = tap_index // 3 - 1
        side_step = tap_index % 3 - 1
        window = padded[
            :, 1 - down_step : 1 - down_step + rows_here, 1 - side_step : 1 - side_step + breadth, :
        ]
        shifted.append(window.reshape(pixels, channels))
    stacked = jnp.stack(shifted, axis=1)
    gathered = lax.all_gather(weights, "dp", axis=1, tiled=True)
    section = lax.all_gather(gathered, "rows", axis=2, tiled=True)
    columns = section.shape[2]
    window = stacked.reshape(pixels, 9 * columns)
    flat = jnp.transpose(section, (0, 2, 1)).reshape(9 * columns, section.shape[1])
    result = jnp.dot(window, flat, preferred_element_type=jnp.float32)
    return result.reshape(images, rows_here, breadth, channels)


def body(
    latent, hidden, cotangent, filter_one, filter_two, gain_one, shift_one, gain_two, shift_two
):
    number = latent.shape[1] * lax.axis_size("rows") * latent.shape[2] * GSIZE
    stats_two = reduced_stats(hidden, number)
    back_two = conv_backward(cotangent, filter_two)
    hidden_grad = norm_backward(hidden, stats_two, gain_two, shift_two, back_two, number).astype(
        jnp.bfloat16
    )
    stats_one = reduced_stats(latent, number)
    back_one = conv_backward(hidden_grad, filter_one)
    latent_part = norm_backward(latent, stats_one, gain_one, shift_one, back_one, number)
    return (cotangent.astype(jnp.float32) + latent_part).astype(jnp.bfloat16)


def solution(mesh):
    in_specs = (
        P("dp", "rows", None, None),
        P("dp", "rows", None, None),
        P("dp", "rows", None, None),
        P(None, "dp", "rows"),
        P(None, "dp", "rows"),
        P(),
        P(),
        P(),
        P(),
    )
    out_specs = P("dp", "rows", None, None)
    return jax.shard_map(body, mesh=mesh, in_specs=in_specs, out_specs=out_specs, check_vma=False)
```

profile of v0, /device:TPU:28, one launch (start us, length us, event | category | flops | bytes accessed | tf_op | source)
XLA Modules:
  0.0 223.1 jit_solution(1200964164859489196)
XLA Ops:
  6.5 1.2 copy.112
  7.7 47.0 %all_gather.12 = bf16[9,640,80]{2,0,1:T(8,128)(2,1)S(1)} all-gather(bf16[9,160,80]{2,0,1:T(8,128)(2,1)S(1)} %copy.112), channel_id=1, replica_groups=mesh['dp'=4,'rows'=8] {'dp'}, dimensions={1}, use_global_device_ids=true | all-gather | bytes 1152000 | tf_op jit(solution)/shard_map/all_gather | solution.py:71
  54.7 3.0 %copy.113 = bf16[9,640,80]{1,2,0:T(8,128)(2,1)} copy(bf16[9,640,80]{2,0,1:T(8,128)(2,1)S(1)} %all_gather.12) | data formatting | bytes 1843200 | tf_op jit(solution)/shard_map/all_gather | solution.py:71
  58.0 45.9 %all_gather.14 = bf16[9,640,80]{2,0,1:T(8,128)(2,1)S(1)} all-gather(bf16[9,160,80]{2,0,1:T(8,128)(2,1)S(1)} %copy.123), channel_id=1, replica_groups=mesh['dp'=4,'rows'=8] {'dp'}, dimensions={1}, use_global_device_ids=true | all-gather | bytes 1152000 | tf_op jit(solution)/shard_map/all_gather | solution.py:71
  103.8 3.0 %copy.124 = bf16[9,640,80]{1,2,0:T(8,128)(2,1)} copy(bf16[9,640,80]{2,0,1:T(8,128)(2,1)S(1)} %all_gather.14) | data formatting | bytes 1843200 | tf_op jit(solution)/shard_map/all_gather | solution.py:71
  106.9 2.1 collective-permute-start
  108.9 4.5 %collective-permute-start.1 = (bf16[2,1,64,640]{3,2,1,0:T(8,128)(2,1)S(1)}, bf16[2,1,64,640]{3,2,1,0:T(8,128)(2,1)S(1)}, u32[]{:S(2)}, u32[]{:S(2)}) collective-permute-start(bf16[2,1,64,640]{3,2,1,0:T(8,128)(2,1)S(1)} %copy-done), channel_id=1, source_target_pairs={{1,0},{2,1},{3,2},{4,3},{5,4},{6,5},{7,6},{9,8},{10,9},{11,10},{12... | collective-permute-start | bytes 491528 | tf_op jit(solution)/shard_map/ppermute | solution.py:18
  113.9 12.3 %all-reduce.4 = (f32[2,16]{1,0:T(2,128)S(1)}, f32[2,16]{1,0:T(2,128)S(1)}) all-reduce(f32[2,16]{1,0:T(2,128)S(1)} %reduce_sum.151, f32[2,16]{1,0:T(2,128)S(1)} %reduce_sum.149), channel_id=1, replica_groups=mesh['dp'=4,'rows'=8] {'rows'}, use_global_device_ids=true, to_apply=%region_11.12 | all-reduce | flops 64 | bytes 512 | tf_op jit(solution)/shard_map/psum | solution.py:40
  132.8 1.0 copy.104
  134.8 11.1 %stack.6 = bf16[128,9,640]{2,1,0:T(8,128)(2,1)S(1)} concatenate(bf16[128,1,640]{2,1,0:T(2,128)(2,1)S(1)} %copy.103, bf16[128,1,640]{2,1,0:T(2,128)(2,1)} %copy.104, bf16[128,1,640]{2,1,0:T(2,128)(2,1)} %copy.105, bf16[128,1,640]{2,1,0:T(2,128)(2,1)} %copy.106, bf16[128,1,640]{2,1,0:T(2,128)(2,1)S(1)} %copy.107, bf16[128,1,640]{2,1,0:T(2,128)(2,1)} %copy.108, ...), dimensions={1} | concatenate | bytes 2949120 | tf_op jit(solution)/shard_map/stack | solution.py:70
  145.9 1.8 reshape.88
  147.7 5.1 %fusion.53 = (f32[2,640]{1,0:T(2,128)S(1)}, f32[2,640]{1,0:T(2,128)S(1)}, f32[2,1,64,640]{3,2,0,1:T(8,128)S(1)}) fusion(f32[2,640]{1,0:T(2,128)S(1)} %mul.122, f32[2,640]{1,0:T(2,128)S(1)} %sub.60, bf16[2,1,64,640]{3,2,1,0:T(8,128)(2,1)S(1)} %copy-done.4, f32[640]{0:T(1024)S(1)} %copy-done.6, f32[640]{0:T(1024)S(1)} %copy-done.7, ...), kind=kOutput, calls=%fused_computation.73 | convolution fusion | flops 945108480 | bytes 9364480 | tf_op jit(solution)/shard_map/dot_general | solution.py:76
  153.1 12.0 %all-reduce.3 = (f32[2,16]{1,0:T(2,128)S(1)}, f32[2,16]{1,0:T(2,128)S(1)}, f32[2,16]{1,0:T(2,128)S(1)}, f32[2,16]{1,0:T(2,128)S(1)}) all-reduce(f32[2,16]{1,0:T(2,128)S(1)} %reduce_sum.155, f32[2,16]{1,0:T(2,128)S(1)} %reduce_sum.153, f32[2,16]{1,0:T(2,128)S(1)} %reduce_sum.147, ...), channel_id=1, replica_groups=mesh['dp'=4,'rows'=8] {'rows'}, use_global_device_ids=true, to_apply=%region_17.18 | all-reduce | flops 128 | bytes 1024 | tf_op jit(solution)/shard_map/psum | solution.py:51
  165.5 1.9 collective-permute-start.2
  167.5 4.7 %collective-permute-start.3 = (bf16[2,1,64,640]{3,2,0,1:T(8,128)(2,1)S(1)}, bf16[2,1,64,640]{3,2,0,1:T(8,128)(2,1)S(1)}, u32[]{:S(2)}, u32[]{:S(2)}) collective-permute-start(bf16[2,1,64,640]{3,2,0,1:T(8,128)(2,1)S(1)} %fusion.50), channel_id=1, source_target_pairs={{1,0},{2,1},{3,2},{4,3},{5,4},{6,5},{7,6},{9,8},{10,9},{11,10},{12... | collective-permute-start | bytes 491528 | tf_op jit(solution)/shard_map/ppermute | solution.py:18
  172.8 1.2 collective-permute-done.2
  175.4 1.0 copy.116
  176.4 1.0 copy.117
  180.3 1.0 copy.115
  181.3 1.0 copy.121
  182.3 11.0 %stack.7 = bf16[128,9,640]{2,1,0:T(8,128)(2,1)S(1)} concatenate(bf16[128,1,640]{2,1,0:T(2,128)(2,1)S(1)} %copy.114, bf16[128,1,640]{2,1,0:T(2,128)(2,1)} %copy.115, bf16[128,1,640]{2,1,0:T(2,128)(2,1)} %copy.116, bf16[128,1,640]{2,1,0:T(2,128)(2,1)} %copy.117, bf16[128,1,640]{2,1,0:T(2,128)(2,1)S(1)} %copy.118, bf16[128,1,640]{2,1,0:T(2,128)(2,1)} %copy.119, ...), dimensions={1} | concatenate | bytes 2949120 | tf_op jit(solution)/shard_map/stack | solution.py:70
  193.4 1.8 reshape.92
  195.2 4.9 %fusion.52 = (f32[2,640]{1,0:T(2,128)S(1)}, f32[2,640]{1,0:T(2,128)S(1)}, f32[2,1,64,640]{3,2,0,1:T(8,128)S(1)}) fusion(f32[2,640]{1,0:T(2,128)S(1)} %mul.118, f32[2,640]{1,0:T(2,128)S(1)} %sub.68, bf16[2,1,64,640]{3,2,1,0:T(8,128)(2,1)S(1)} %copy-done.2, f32[640]{0:T(1024)S(1)} %copy-done.8, f32[640]{0:T(1024)S(1)} %copy-done.9, ...), kind=kOutput, calls=%fused_computation.72 | convolution fusion | flops 945108480 | bytes 9364480 | tf_op jit(solution)/shard_map/dot_general | solution.py:76
  200.5 14.6 %all-reduce.2 = (f32[2,16]{1,0:T(2,128)S(1)}, f32[2,16]{1,0:T(2,128)S(1)}) all-reduce(f32[2,16]{1,0:T(2,128)S(1)} %reduce_sum.159, f32[2,16]{1,0:T(2,128)S(1)} %reduce_sum.157), channel_id=1, replica_groups=mesh['dp'=4,'rows'=8] {'rows'}, use_global_device_ids=true, to_apply=%region_23.24 | all-reduce | flops 64 | bytes 512 | tf_op jit(solution)/shard_map/psum | solution.py:51
  (88 shorter events, 15.3 us)
Async XLA Ops:
  6.5 141.2 %all-gather.3.cloned.1.call-start = ((), (), s32[]{:S(2)}) async-start(), calls=%async_computation | async-start | bytes 8294400 | tf_op jit(solution)/shard_map/all_gather | solution.py:72
  54.7 3.1 %copy-start.5 = (bf16[9,160,80]{2,1,0:T(8,128)(2,1)S(1)}, bf16[9,160,80]{2,1,0:T(8,128)(2,1)}, u32[]{:S(2)}) copy-start(bf16[9,160,80]{2,1,0:T(8,128)(2,1)} %param.12) | copy-start | bytes 691204
  57.7 137.5 %all-gather.5.cloned.1.call-start = ((), (), s32[]{:S(2)}) async-start(), calls=%async_computation.1 | async-start | bytes 8294400 | tf_op jit(solution)/shard_map/all_gather | solution.py:72
  103.8 3.0 %copy-start = (bf16[2,1,64,640]{3,2,1,0:T(8,128)(2,1)S(1)}, bf16[2,1,64,640]{3,2,1,0:T(8,128)(2,1)}, u32[]{:S(2)}) copy-start(bf16[2,1,64,640]{3,2,1,0:T(8,128)(2,1)} %param.11) | copy-start | bytes 491524
  103.8 9.6 %copy-start.3 = (bf16[2,1,64,640]{3,2,1,0:T(8,128)(2,1)S(1)}, bf16[2,1,64,640]{3,2,1,0:T(8,128)(2,1)}, u32[]{:S(2)}) copy-start(bf16[2,1,64,640]{3,2,1,0:T(8,128)(2,1)} %param.10) | copy-start | bytes 491524
  106.8 20.0 %copy-start.1 = (bf16[2,1,64,640]{3,2,1,0:T(8,128)(2,1)S(1)}, bf16[2,1,64,640]{3,2,1,0:T(8,128)(2,1)}, u32[]{:S(2)}) copy-start(bf16[2,1,64,640]{3,2,1,0:T(8,128)(2,1)} %param.9) | copy-start | bytes 491524
  106.9 20.4 %collective-permute-start = (bf16[2,1,64,640]{3,2,1,0:T(8,128)(2,1)S(1)}, bf16[2,1,64,640]{3,2,1,0:T(8,128)(2,1)S(1)}, u32[]{:S(2)}, u32[]{:S(2)}) collective-permute-start(bf16[2,1,64,640]{3,2,1,0:T(8,128)(2,1)S(1)} %copy-done), channel_id=1, source_target_pairs={{0,1},{1,2},{2,3},{3,4},{4,5},{5,6},{6,7},{8,9},{9,10},{10,11},{11... | collective-permute-start | bytes 491528 | tf_op jit(solution)/shard_map/ppermute | solution.py:15
  108.9 18.4 %collective-permute-start.1 = (bf16[2,1,64,640]{3,2,1,0:T(8,128)(2,1)S(1)}, bf16[2,1,64,640]{3,2,1,0:T(8,128)(2,1)S(1)}, u32[]{:S(2)}, u32[]{:S(2)}) collective-permute-start(bf16[2,1,64,640]{3,2,1,0:T(8,128)(2,1)S(1)} %copy-done), channel_id=1, source_target_pairs={{1,0},{2,1},{3,2},{4,3},{5,4},{6,5},{7,6},{9,8},{10,9},{11,10},{12... | collective-permute-start | bytes 491528 | tf_op jit(solution)/shard_map/ppermute | solution.py:18
  145.9 1.8 copy-start.4
  145.9 1.8 copy-start.6
  145.9 1.8 copy-start.7
  165.5 8.4 %collective-permute-start.2 = (bf16[2,1,64,640]{3,2,0,1:T(8,128)(2,1)S(1)}, bf16[2,1,64,640]{3,2,0,1:T(8,128)(2,1)S(1)}, u32[]{:S(2)}, u32[]{:S(2)}) collective-permute-start(bf16[2,1,64,640]{3,2,0,1:T(8,128)(2,1)S(1)} %fusion.50), channel_id=1, source_target_pairs={{0,1},{1,2},{2,3},{3,4},{4,5},{5,6},{6,7},{8,9},{9,10},{10,11},{11... | collective-permute-start | bytes 491528 | tf_op jit(solution)/shard_map/ppermute | solution.py:15
  167.5 7.4 %collective-permute-start.3 = (bf16[2,1,64,640]{3,2,0,1:T(8,128)(2,1)S(1)}, bf16[2,1,64,640]{3,2,0,1:T(8,128)(2,1)S(1)}, u32[]{:S(2)}, u32[]{:S(2)}) collective-permute-start(bf16[2,1,64,640]{3,2,0,1:T(8,128)(2,1)S(1)} %fusion.50), channel_id=1, source_target_pairs={{1,0},{2,1},{3,2},{4,3},{5,4},{6,5},{7,6},{9,8},{10,9},{11,10},{12... | collective-permute-start | bytes 491528 | tf_op jit(solution)/shard_map/ppermute | solution.py:18
  193.4 1.8 copy-start.2
  193.4 1.8 copy-start.8
  193.4 1.8 copy-start.9
Sparse Core Ops, SparseCore 0:
  57.9 50.5 all-gather.2
  110.4 50.1 all-gather.4
where the time goes:
time: 225 us; the launch traced here: 223 us
  blocking collectives  132 us (59%)
  local copies, waits for them, and re-layouts  50.2 us (22%)
  between operations  13.8 us (6%)
  starting transfers between devices  13.3 us (6%)
  matrix products  10 us (4%)
    all_gather x2, blocking collectives, conv_backward(): gathered = lax.all_gather(weights, 'dp', axis=1, tiled=True)  92.9 us
    another operation x20, local copies, waits for them, and re-layouts, conv_backward(): stacked = jnp.stack(shifted, axis=1)  36.9 us
    psum x2, blocking collectives, norm_backward(): lax.psum((group_sums(scaled), group_sums(scaled * normed)), 'rows')  26.5 us
    psum x1, blocking collectives, reduced_stats(): lax.psum((group_sums(values), group_sums(values * values)), 'rows')  12.3 us
    dot_general x2, matrix products, conv_backward(): result = jnp.dot(window, flat, preferred_element_type=jnp.float32)  10 us
    ppermute x2, starting transfers between devices, extended(): lax.ppermute(lax.slice_in_dim(block, 0, width, axis=dim), axis, backward)  9.26 us
    all_gather x2, local copies, waits for them, and re-layouts, conv_backward(): gathered = lax.all_gather(weights, 'dp', axis=1, tiled=True)  5.97 us
  transfers between devices with their start and end apart: 6, of which 2 were waited for; matrix products, arithmetic and copies ran while one was open for 23% of the time, Pallas kernels for 0%

commit v1 on v0

--- a/solution.py
+++ b/solution.py
@@ -68,7 +68,23 @@
         ]
         shifted.append(window.reshape(pixels, channels))
     stacked = jnp.stack(shifted, axis=1)
-    gathered = lax.all_gather(weights, "dp", axis=1, tiled=True)
+
+    def divide_samples_for(content, ax_name):
+        n_lanes = lax.axis_size(ax_name)
+        near = [(num - 1, num) for num in range(1, n_lanes)] + [(n_lanes - 1, 0)]
+        work_now = content
+        nodes = [work_now]
+        to_i = 0
+        while to_i < n_lanes - 1:
+            work_now = lax.ppermute(work_now, axis_name=ax_name, perm=near)
+            nodes += [work_now]
+            to_i += 1
+        x_next = jnp.concatenate([*reversed(nodes)], axis=1)
+        extra = lax.axis_index(ax_name)
+        lower = jnp.roll(x_next, (extra + 1) * work_now.shape[1], axis=1)
+        return lower
+
+    gathered = divide_samples_for(weights, "dp")
     section = lax.all_gather(gathered, "rows", axis=2, tiled=True)
     columns = section.shape[2]
     window = stacked.reshape(pixels, 9 * columns)

time: 225 us -> 200 us (0.89)
  the two profiles are of different devices: /device:TPU:28 before, /device:TPU:4 now
where the time goes in v1:
time: 200 us; the launch traced here: 198 us
  waiting for transfers between devices  67.7 us (34%)
  local copies, waits for them, and re-layouts  44.2 us (22%)
  blocking collectives  40.4 us (20%)
  between operations  13.8 us (7%)
  other arithmetic  11.6 us (6%)
  starting transfers between devices  10.4 us (5%)
  matrix products  9.88 us (5%)
    ppermute x6, waiting for transfers between devices, divide_samples_for(): work_now = lax.ppermute(work_now, axis_name=ax_name, perm=near)  60.9 us
    another operation x20, local copies, waits for them, and re-layouts, conv_backward(): stacked = jnp.stack(shifted, axis=1)  36.9 us
    psum x2, blocking collectives, norm_backward(): lax.psum((group_sums(scaled), group_sums(scaled * normed)), 'rows')  25.1 us
    psum x1, blocking collectives, reduced_stats(): lax.psum((group_sums(values), group_sums(values * values)), 'rows')  15.3 us
    dot_general x2, matrix products, conv_backward(): result = jnp.dot(window, flat, preferred_element_type=jnp.float32)  9.88 us
    concatenate x2, other arithmetic, divide_samples_for(): lower = jnp.roll(x_next, (extra + 1) * work_now.shape[1], axis=1)  9.51 us
    ppermute x2, starting transfers between devices, extended(): lax.ppermute(lax.slice_in_dim(block, block.shape[dim] - width, None, axis...  4.81 us
    ppermute x2, waiting for transfers between devices, extended(): lax.ppermute(lax.slice_in_dim(block, 0, width, axis=dim), axis, backward)  4.14 us
  transfers between devices with their start and end apart: 12, of which 8 were waited for; matrix products, arithmetic and copies ran while one was open for 27% of the time, Pallas kernels for 0%

profile of v1, /device:TPU:4, one launch (start us, length us, event | category | flops | bytes accessed | tf_op | source)
XLA Modules:
  0.0 197.9 jit_solution(2430553926243509620)
XLA Ops:
  7.8 1.6 collective-permute-start.2
  9.4 10.6 %collective-permute-done.2 = bf16[9,160,80]{1,2,0:T(8,128)(2,1)S(1)} collective-permute-done((bf16[9,160,80]{1,2,0:T(8,128)(2,1)S(1)}, bf16[9,160,80]{1,2,0:T(8,128)(2,1)S(1)}, u32[]{:S(2)}, u32[]{:S(2)}) %collective-permute-start.2) | collective-permute-done | bytes 230432 | tf_op jit(solution)/shard_map/ppermute | solution.py:79
  20.0 11.3 %collective-permute-done.3 = bf16[9,160,80]{1,2,0:T(8,128)(2,1)S(1)} collective-permute-done((bf16[9,160,80]{1,2,0:T(8,128)(2,1)S(1)}, bf16[9,160,80]{1,2,0:T(8,128)(2,1)S(1)}, u32[]{:S(2)}, u32[]{:S(2)}) %collective-permute-start.3) | collective-permute-done | bytes 230432 | tf_op jit(solution)/shard_map/ppermute | solution.py:79
  31.3 10.5 %collective-permute-done.4 = bf16[9,160,80]{1,2,0:T(8,128)(2,1)S(1)} collective-permute-done((bf16[9,160,80]{1,2,0:T(8,128)(2,1)S(1)}, bf16[9,160,80]{1,2,0:T(8,128)(2,1)S(1)}, u32[]{:S(2)}, u32[]{:S(2)}) %collective-permute-start.4) | collective-permute-done | bytes 230432 | tf_op jit(solution)/shard_map/ppermute | solution.py:79
  41.8 4.8 %fusion.18 = bf16[9,640,80]{1,2,0:T(8,128)(2,1)} fusion(s32[]{:T(128)S(6)} %select_n.13, bf16[9,160,80]{1,2,0:T(8,128)(2,1)S(1)} %collective-permute-done.4, bf16[9,160,80]{1,2,0:T(8,128)(2,1)S(1)} %collective-permute-done.3, bf16[9,160,80]{1,2,0:T(8,128)(2,1)S(1)} %collective-permute-done.2, bf16[9,160,80]{1,2,0:T(8,128)(2,1)S(1)} %copy.88), kind=kLoop, calls=%fused_computation.40 | loop fusion | flops 7372800 | bytes 1843204 | tf_op jit(solution)/shard_map/jit(_roll_dynamic)/concatenate | solution.py:84
  47.0 9.6 %collective-permute-done.7 = bf16[9,160,80]{1,2,0:T(8,128)(2,1)S(1)} collective-permute-done((bf16[9,160,80]{1,2,0:T(8,128)(2,1)S(1)}, bf16[9,160,80]{1,2,0:T(8,128)(2,1)S(1)}, u32[]{:S(2)}, u32[]{:S(2)}) %collective-permute-start.7) | collective-permute-done | bytes 230432 | tf_op jit(solution)/shard_map/ppermute | solution.py:79
  56.6 9.6 %collective-permute-done.8 = bf16[9,160,80]{1,2,0:T(8,128)(2,1)S(1)} collective-permute-done((bf16[9,160,80]{1,2,0:T(8,128)(2,1)S(1)}, bf16[9,160,80]{1,2,0:T(8,128)(2,1)S(1)}, u32[]{:S(2)}, u32[]{:S(2)}) %collective-permute-start.8) | collective-permute-done | bytes 230432 | tf_op jit(solution)/shard_map/ppermute | solution.py:79
  66.2 9.3 %collective-permute-done.9 = bf16[9,160,80]{1,2,0:T(8,128)(2,1)S(1)} collective-permute-done((bf16[9,160,80]{1,2,0:T(8,128)(2,1)S(1)}, bf16[9,160,80]{1,2,0:T(8,128)(2,1)S(1)}, u32[]{:S(2)}, u32[]{:S(2)}) %collective-permute-start.9) | collective-permute-done | bytes 230432 | tf_op jit(solution)/shard_map/ppermute | solution.py:79
  75.5 4.7 %fusion.11 = bf16[9,640,80]{1,2,0:T(8,128)(2,1)} fusion(s32[]{:T(128)S(6)} %select_n.13, bf16[9,160,80]{1,2,0:T(8,128)(2,1)S(1)} %collective-permute-done.9, bf16[9,160,80]{1,2,0:T(8,128)(2,1)S(1)} %collective-permute-done.8, bf16[9,160,80]{1,2,0:T(8,128)(2,1)S(1)} %collective-permute-done.7, bf16[9,160,80]{1,2,0:T(8,128)(2,1)S(1)} %copy.99), kind=kLoop, calls=%fused_computation.33 | loop fusion | flops 7372800 | bytes 1843204 | tf_op jit(solution)/shard_map/jit(_roll_dynamic)/concatenate | solution.py:84
  80.3 1.9 collective-permute-start.1
  82.2 2.4 %collective-permute-start = (bf16[2,1,64,640]{3,2,1,0:T(8,128)(2,1)S(1)}, bf16[2,1,64,640]{3,2,1,0:T(8,128)(2,1)S(1)}, u32[]{:S(2)}, u32[]{:S(2)}) collective-permute-start(bf16[2,1,64,640]{3,2,1,0:T(8,128)(2,1)S(1)} %copy-done), channel_id=1, source_target_pairs={{0,1},{1,2},{2,3},{3,4},{4,5},{5,6},{6,7},{8,9},{9,10},{10,11},{11... | collective-permute-start | bytes 491528 | tf_op jit(solution)/shard_map/ppermute | solution.py:15
  85.1 15.3 %all-reduce.4 = (f32[2,16]{1,0:T(2,128)S(1)}, f32[2,16]{1,0:T(2,128)S(1)}) all-reduce(f32[2,16]{1,0:T(2,128)S(1)} %reduce_sum.151, f32[2,16]{1,0:T(2,128)S(1)} %reduce_sum.149), channel_id=1, replica_groups=mesh['dp'=4,'rows'=8] {'rows'}, use_global_device_ids=true, to_apply=%region_11.12 | all-reduce | flops 64 | bytes 512 | tf_op jit(solution)/shard_map/psum | solution.py:40
  108.9 11.0 %stack.6 = bf16[128,9,640]{2,1,0:T(8,128)(2,1)S(1)} concatenate(bf16[128,1,640]{2,1,0:T(2,128)(2,1)S(1)} %copy.79, bf16[128,1,640]{2,1,0:T(2,128)(2,1)} %copy.80, bf16[128,1,640]{2,1,0:T(2,128)(2,1)} %copy.81, bf16[128,1,640]{2,1,0:T(2,128)(2,1)} %copy.82, bf16[128,1,640]{2,1,0:T(2,128)(2,1)S(1)} %copy.83, bf16[128,1,640]{2,1,0:T(2,128)(2,1)} %copy.84, ...), dimensions={1} | concatenate | bytes 2949120 | tf_op jit(solution)/shard_map/stack | solution.py:70
  120.0 1.8 reshape.88
  121.8 4.9 %fusion.67 = (f32[2,640]{1,0:T(2,128)S(1)}, f32[2,640]{1,0:T(2,128)S(1)}, f32[2,1,64,640]{3,2,0,1:T(8,128)S(1)}) fusion(f32[2,640]{1,0:T(2,128)S(1)} %mul.126, f32[2,640]{1,0:T(2,128)S(1)} %sub.63, bf16[2,1,64,640]{3,2,1,0:T(8,128)(2,1)S(1)} %copy-done.4, f32[640]{0:T(1024)S(1)} %copy-done.6, f32[640]{0:T(1024)S(1)} %copy-done.7, ...), kind=kOutput, calls=%fused_computation.103 | convolution fusion | flops 945108480 | bytes 9364480 | tf_op jit(solution)/shard_map/dot_general | solution.py:92
  127.1 13.1 %all-reduce.3 = (f32[2,16]{1,0:T(2,128)S(1)}, f32[2,16]{1,0:T(2,128)S(1)}, f32[2,16]{1,0:T(2,128)S(1)}, f32[2,16]{1,0:T(2,128)S(1)}) all-reduce(f32[2,16]{1,0:T(2,128)S(1)} %reduce_sum.155, f32[2,16]{1,0:T(2,128)S(1)} %reduce_sum.153, f32[2,16]{1,0:T(2,128)S(1)} %reduce_sum.147, ...), channel_id=1, replica_groups=mesh['dp'=4,'rows'=8] {'rows'}, use_global_device_ids=true, to_apply=%region_17.19 | all-reduce | flops 128 | bytes 1024 | tf_op jit(solution)/shard_map/psum | solution.py:51
  140.6 1.9 collective-permute-start.6
  142.6 2.4 %collective-permute-start.5 = (bf16[2,1,64,640]{3,2,0,1:T(8,128)(2,1)S(1)}, bf16[2,1,64,640]{3,2,0,1:T(8,128)(2,1)S(1)}, u32[]{:S(2)}, u32[]{:S(2)}) collective-permute-start(bf16[2,1,64,640]{3,2,0,1:T(8,128)(2,1)S(1)} %fusion.64), channel_id=1, source_target_pairs={{0,1},{1,2},{2,3},{3,4},{4,5},{5,6},{6,7},{8,9},{9,10},{10,11},{11... | collective-permute-start | bytes 491528 | tf_op jit(solution)/shard_map/ppermute | solution.py:15
  145.6 4.1 %collective-permute-done.6 = bf16[2,1,64,640]{3,2,0,1:T(8,128)(2,1)S(1)} collective-permute-done((bf16[2,1,64,640]{3,2,0,1:T(8,128)(2,1)S(1)}, bf16[2,1,64,640]{3,2,0,1:T(8,128)(2,1)S(1)}, u32[]{:S(2)}, u32[]{:S(2)}) %collective-permute-start.6) | collective-permute-done | bytes 163872 | tf_op jit(solution)/shard_map/ppermute | solution.py:18
  149.7 2.6 %collective-permute-done.5 = bf16[2,1,64,640]{3,2,0,1:T(8,128)(2,1)S(1)} collective-permute-done((bf16[2,1,64,640]{3,2,0,1:T(8,128)(2,1)S(1)}, bf16[2,1,64,640]{3,2,0,1:T(8,128)(2,1)S(1)}, u32[]{:S(2)}, u32[]{:S(2)}) %collective-permute-start.5) | collective-permute-done | bytes 163872 | tf_op jit(solution)/shard_map/ppermute | solution.py:15
  159.8 11.0 %stack.7 = bf16[128,9,640]{2,1,0:T(8,128)(2,1)S(1)} concatenate(bf16[128,1,640]{2,1,0:T(2,128)(2,1)S(1)} %copy.90, bf16[128,1,640]{2,1,0:T(2,128)(2,1)} %copy.91, bf16[128,1,640]{2,1,0:T(2,128)(2,1)} %copy.92, bf16[128,1,640]{2,1,0:T(2,128)(2,1)} %copy.93, bf16[128,1,640]{2,1,0:T(2,128)(2,1)S(1)} %copy.94, bf16[128,1,640]{2,1,0:T(2,128)(2,1)} %copy.95, ...), dimensions={1} | concatenate | bytes 2949120 | tf_op jit(solution)/shard_map/stack | solution.py:70
  170.9 1.8 reshape.92
  172.7 4.9 %fusion.66 = (f32[2,640]{1,0:T(2,128)S(1)}, f32[2,640]{1,0:T(2,128)S(1)}, f32[2,1,64,640]{3,2,0,1:T(8,128)S(1)}) fusion(f32[2,640]{1,0:T(2,128)S(1)} %mul.122, f32[2,640]{1,0:T(2,128)S(1)} %sub.71, bf16[2,1,64,640]{3,2,1,0:T(8,128)(2,1)S(1)} %copy-done.2, f32[640]{0:T(1024)S(1)} %copy-done.8, f32[640]{0:T(1024)S(1)} %copy-done.9, ...), kind=kOutput, calls=%fused_computation.102 | convolution fusion | flops 945108480 | bytes 9364480 | tf_op jit(solution)/shard_map/dot_general | solution.py:92
  178.0 12.0 %all-reduce.2 = (f32[2,16]{1,0:T(2,128)S(1)}, f32[2,16]{1,0:T(2,128)S(1)}) all-reduce(f32[2,16]{1,0:T(2,128)S(1)} %reduce_sum.159, f32[2,16]{1,0:T(2,128)S(1)} %reduce_sum.157), channel_id=1, replica_groups=mesh['dp'=4,'rows'=8] {'rows'}, use_global_device_ids=true, to_apply=%region_23.25 | all-reduce | flops 64 | bytes 512 | tf_op jit(solution)/shard_map/psum | solution.py:51
  (98 shorter events, 20.8 us)
Async XLA Ops:
  6.5 115.2 %all-gather.3.cloned.1.call-start = ((), (), s32[]{:S(2)}) async-start(), calls=%async_computation | async-start | bytes 8294400 | tf_op jit(solution)/shard_map/all_gather | solution.py:88
  7.8 38.9 %copy-start.5 = (bf16[9,160,80]{2,1,0:T(8,128)(2,1)S(1)}, bf16[9,160,80]{2,1,0:T(8,128)(2,1)}, u32[]{:S(2)}) copy-start(bf16[9,160,80]{2,1,0:T(8,128)(2,1)} %param.14) | copy-start | bytes 691204
  7.8 12.2 %collective-permute-start.2 = (bf16[9,160,80]{1,2,0:T(8,128)(2,1)S(1)}, bf16[9,160,80]{1,2,0:T(8,128)(2,1)S(1)}, u32[]{:S(2)}, u32[]{:S(2)}) collective-permute-start(bf16[9,160,80]{1,2,0:T(8,128)(2,1)S(1)} %copy.88), channel_id=1, source_target_pairs={{0,8},{8,16},{16,24},{24,0},{1,9},{9,17},{17,25},{25,1},{2,10},{10... | collective-permute-start | bytes 691208 | tf_op jit(solution)/shard_map/ppermute | solution.py:79
  20.0 11.3 %collective-permute-start.3 = (bf16[9,160,80]{1,2,0:T(8,128)(2,1)S(1)}, bf16[9,160,80]{1,2,0:T(8,128)(2,1)S(1)}, u32[]{:S(2)}, u32[]{:S(2)}) collective-permute-start(bf16[9,160,80]{1,2,0:T(8,128)(2,1)S(1)} %collective-permute-done.2), channel_id=1, source_target_pairs={{0,8},{8,16},{16,24},{24,0},{1,9},{9,17},{17,25},{25,1},{2,10},{10... | collective-permute-start | bytes 691208 | tf_op jit(solution)/shard_map/ppermute | solution.py:79
  31.3 10.5 %collective-permute-start.4 = (bf16[9,160,80]{1,2,0:T(8,128)(2,1)S(1)}, bf16[9,160,80]{1,2,0:T(8,128)(2,1)S(1)}, u32[]{:S(2)}, u32[]{:S(2)}) collective-permute-start(bf16[9,160,80]{1,2,0:T(8,128)(2,1)S(1)} %collective-permute-done.3), channel_id=1, source_target_pairs={{0,8},{8,16},{16,24},{24,0},{1,9},{9,17},{17,25},{25,1},{2,10},{10... | collective-permute-start | bytes 691208 | tf_op jit(solution)/shard_map/ppermute | solution.py:79
  46.6 126.1 %all-gather.5.cloned.1.call-start = ((), (), s32[]{:S(2)}) async-start(), calls=%async_computation.1 | async-start | bytes 8294400 | tf_op jit(solution)/shard_map/all_gather | solution.py:88
  46.9 33.4 %copy-start = (bf16[2,1,64,640]{3,2,1,0:T(8,128)(2,1)S(1)}, bf16[2,1,64,640]{3,2,1,0:T(8,128)(2,1)}, u32[]{:S(2)}) copy-start(bf16[2,1,64,640]{3,2,1,0:T(8,128)(2,1)} %param.13) | copy-start | bytes 491524
  46.9 37.7 %copy-start.3 = (bf16[2,1,64,640]{3,2,1,0:T(8,128)(2,1)S(1)}, bf16[2,1,64,640]{3,2,1,0:T(8,128)(2,1)}, u32[]{:S(2)}) copy-start(bf16[2,1,64,640]{3,2,1,0:T(8,128)(2,1)} %param.12) | copy-start | bytes 491524
  46.9 54.1 %copy-start.1 = (bf16[2,1,64,640]{3,2,1,0:T(8,128)(2,1)S(1)}, bf16[2,1,64,640]{3,2,1,0:T(8,128)(2,1)}, u32[]{:S(2)}) copy-start(bf16[2,1,64,640]{3,2,1,0:T(8,128)(2,1)} %param.11) | copy-start | bytes 491524
  46.9 9.7 %collective-permute-start.7 = (bf16[9,160,80]{1,2,0:T(8,128)(2,1)S(1)}, bf16[9,160,80]{1,2,0:T(8,128)(2,1)S(1)}, u32[]{:S(2)}, u32[]{:S(2)}) collective-permute-start(bf16[9,160,80]{1,2,0:T(8,128)(2,1)S(1)} %copy.99), channel_id=1, source_target_pairs={{0,8},{8,16},{16,24},{24,0},{1,9},{9,17},{17,25},{25,1},{2,10},{10... | collective-permute-start | bytes 691208 | tf_op jit(solution)/shard_map/ppermute | solution.py:79
  56.6 9.6 %collective-permute-start.8 = (bf16[9,160,80]{1,2,0:T(8,128)(2,1)S(1)}, bf16[9,160,80]{1,2,0:T(8,128)(2,1)S(1)}, u32[]{:S(2)}, u32[]{:S(2)}) collective-permute-start(bf16[9,160,80]{1,2,0:T(8,128)(2,1)S(1)} %collective-permute-done.7), channel_id=1, source_target_pairs={{0,8},{8,16},{16,24},{24,0},{1,9},{9,17},{17,25},{25,1},{2,10},{10... | collective-permute-start | bytes 691208 | tf_op jit(solution)/shard_map/ppermute | solution.py:79
  66.2 9.3 %collective-permute-start.9 = (bf16[9,160,80]{1,2,0:T(8,128)(2,1)S(1)}, bf16[9,160,80]{1,2,0:T(8,128)(2,1)S(1)}, u32[]{:S(2)}, u32[]{:S(2)}) collective-permute-start(bf16[9,160,80]{1,2,0:T(8,128)(2,1)S(1)} %collective-permute-done.8), channel_id=1, source_target_pairs={{0,8},{8,16},{16,24},{24,0},{1,9},{9,17},{17,25},{25,1},{2,10},{10... | collective-permute-start | bytes 691208 | tf_op jit(solution)/shard_map/ppermute | solution.py:79
  80.3 21.2 %collective-permute-start.1 = (bf16[2,1,64,640]{3,2,1,0:T(8,128)(2,1)S(1)}, bf16[2,1,64,640]{3,2,1,0:T(8,128)(2,1)S(1)}, u32[]{:S(2)}, u32[]{:S(2)}) collective-permute-start(bf16[2,1,64,640]{3,2,1,0:T(8,128)(2,1)S(1)} %copy-done), channel_id=1, source_target_pairs={{1,0},{2,1},{3,2},{4,3},{5,4},{6,5},{7,6},{9,8},{10,9},{11,10},{12... | collective-permute-start | bytes 491528 | tf_op jit(solution)/shard_map/ppermute | solution.py:18
  82.2 19.2 %collective-permute-start = (bf16[2,1,64,640]{3,2,1,0:T(8,128)(2,1)S(1)}, bf16[2,1,64,640]{3,2,1,0:T(8,128)(2,1)S(1)}, u32[]{:S(2)}, u32[]{:S(2)}) collective-permute-start(bf16[2,1,64,640]{3,2,1,0:T(8,128)(2,1)S(1)} %copy-done), channel_id=1, source_target_pairs={{0,1},{1,2},{2,3},{3,4},{4,5},{5,6},{6,7},{8,9},{9,10},{10,11},{11... | collective-permute-start | bytes 491528 | tf_op jit(solution)/shard_map/ppermute | solution.py:15
  119.9 1.8 copy-start.4
  120.0 1.8 copy-start.6
  120.0 1.8 copy-start.7
  140.6 9.1 %collective-permute-start.6 = (bf16[2,1,64,640]{3,2,0,1:T(8,128)(2,1)S(1)}, bf16[2,1,64,640]{3,2,0,1:T(8,128)(2,1)S(1)}, u32[]{:S(2)}, u32[]{:S(2)}) collective-permute-start(bf16[2,1,64,640]{3,2,0,1:T(8,128)(2,1)S(1)} %fusion.64), channel_id=1, source_target_pairs={{1,0},{2,1},{3,2},{4,3},{5,4},{6,5},{7,6},{9,8},{10,9},{11,10},{12... | collective-permute-start | bytes 491528 | tf_op jit(solution)/shard_map/ppermute | solution.py:18
  142.6 9.7 %collective-permute-start.5 = (bf16[2,1,64,640]{3,2,0,1:T(8,128)(2,1)S(1)}, bf16[2,1,64,640]{3,2,0,1:T(8,128)(2,1)S(1)}, u32[]{:S(2)}, u32[]{:S(2)}) collective-permute-start(bf16[2,1,64,640]{3,2,0,1:T(8,128)(2,1)S(1)} %fusion.64), channel_id=1, source_target_pairs={{0,1},{1,2},{2,3},{3,4},{4,5},{5,6},{6,7},{8,9},{9,10},{10,11},{11... | collective-permute-start | bytes 491528 | tf_op jit(solution)/shard_map/ppermute | solution.py:15
  170.8 1.8 copy-start.2
  170.8 1.8 copy-start.8
  170.9 1.8 copy-start.9
Sparse Core Ops, SparseCore 0:
  46.7 49.7 all-gather.2
  98.4 53.7 all-gather.4
